TPU v7x, 32 devices: a whole 2x2x4 slice. The times are simulated.
32 devices in a mesh: expert: 4 (over y, core), shard: 8 (over z, x).
Axes of the slice: x: 2, y: 2, z: 4, core: 2. Of those that a mesh axis runs over, the one named last changes fastest.
Arguments:
- master_gate: float32 [128, 2048, 768], P('expert', 'shard'), may hold values from -0.125 to 0.125
- second_gate: bfloat16 [128, 2048, 768], P('expert', 'shard'), may hold values from -0.0625 to 0.0625
- master_up: float32 [128, 2048, 768], P('expert', 'shard'), may hold values from -0.125 to 0.125
- second_up: bfloat16 [128, 2048, 768], P('expert', 'shard'), may hold values from -0.0625 to 0.0625
- router_weight: float32 [2048, 128], P('shard', 'expert'), may hold values from -0.125 to 0.125
- router_gain: float32 [2048], P('shard'), may hold values from 0.25 to 1.75
Outputs:
- final_gate: bfloat16 [128, 768, 2048], P('expert', 'shard')
- final_up: bfloat16 [128, 768, 2048], P('expert', 'shard')
- serve_router: bfloat16 [2048, 128], replicated
All inputs are finite; a program needn't handle non-finite values.
Results may differ from a plain program's by a relative error of at most 0.001.
Values may be sent and summed in bfloat16 or wider, within the bound.
A program may use at most 192 MiB of HBM per device.

v0:
```python
import functools

import jax
import jax.numpy as jnp
from jax import lax
from jax.experimental import pallas as pl
from jax.experimental.pallas import tpu as pltpu
from jax.sharding import PartitionSpec as P

MESH = pl.DeviceIdType.MESH
SLOTS = 3
ORDER = 0


def exchange_kernel(
    n, groups, mg, sg, mu, su, part, recv, router,
    wide, narrow, outbox, in_sem, send_sem, recv_sem, own_sem, rs_send, rs_recv, re_send, re_recv,
):
    experts, rows, _ = mg.shape
    block = outbox.shape[3]
    columns = part.shape[0]
    me = lax.axis_index("shard")
    group = lax.axis_index("expert")

    def load(e):
        slot = lax.rem(e, SLOTS)
        return (
            pltpu.make_async_copy(mg.at[e], wide.at[slot, 0], in_sem.at[slot, 0]),
            pltpu.make_async_copy(sg.at[e], narrow.at[slot, 0], in_sem.at[slot, 1]),
            pltpu.make_async_copy(mu.at[e], wide.at[slot, 1], in_sem.at[slot, 2]),
            pltpu.make_async_copy(su.at[e], narrow.at[slot, 1], in_sem.at[slot, 3]),
        )

    for e in range(SLOTS):
        for copy in load(e):
            copy.start()

    barrier = pltpu.get_barrier_semaphore()
    for j in range(1, n):
        pl.semaphore_signal(barrier, inc=1, device_id=(group, lax.rem(me + j, n)), device_id_type=MESH)
    for j in range(1, groups):
        pl.semaphore_signal(barrier, inc=1, device_id=(lax.rem(group + j, groups), me), device_id_type=MESH)
    pl.semaphore_wait(barrier, n - 1 + groups - 1)

    band = router.at[pl.ds(pl.multiple_of(group * columns, columns), columns)]
    spot = band.at[:, pl.ds(pl.multiple_of(me * rows, rows), rows)]
    own_router = pltpu.make_async_copy(part, spot, own_sem.at[1])
    own_router.start()
    router_rows = []
    for j in range(1, n):
        router_rows.append(
            pltpu.make_async_remote_copy(
                src_ref=part, dst_ref=spot, send_sem=rs_send.at[j], recv_sem=rs_recv.at[j],
                device_id=(group, lax.rem(me + j, n)), device_id_type=MESH,
            )
        )
        router_rows[-1].start()

    half, quarter = n // 2, max(n // 4, 1)
    lower = me < half
    outer = jnp.logical_or(me < quarter, me >= n - quarter)
    near = [lax.rem(me + j, half) + jnp.where(lower, 0, half) for j in range(1, half)]
    far = [lax.rem(me + j, half) + jnp.where(lower, half, 0) for j in range(half)]

    def send(e, peer):
        pltpu.make_async_remote_copy(
            src_ref=outbox.at[peer, e], dst_ref=recv.at[me, e],
            send_sem=send_sem.at[peer], recv_sem=recv_sem.at[me],
            device_id=(group, peer), device_id_type=MESH,
        ).start()

    def send_first(e):
        if ORDER == 0:
            for peer in far + near:
                send(e, peer)
        elif ORDER == 1:
            for peer in near + far:
                send(e, peer)
        else:
            @pl.when(outer)
            def _():
                for peer in near:
                    send(e, peer)

            @pl.when(jnp.logical_not(outer))
            def _():
                for peer in far:
                    send(e, peer)

    def send_second(e):
        @pl.when(outer)
        def _():
            for peer in far:
                send(e, peer)

        @pl.when(jnp.logical_not(outer))
        def _():
            for peer in near:
                send(e, peer)

    def step(e, _):
        slot = lax.rem(e, SLOTS)
        for copy in load(e):
            copy.wait()
        for which in range(2):
            merged = wide[slot, which] + narrow[slot, which].astype(jnp.float32)
            turned = merged.astype(jnp.bfloat16).T
            for d in range(n):
                outbox[d, e, which] = turned[d * block:(d + 1) * block]

        @pl.when(e + SLOTS < experts)
        def _():
            for copy in load(e + SLOTS):
                copy.start()

        @pl.when(e > 0)
        def _():
            send_first(e - 1)

        return 0

    lax.fori_loop(0, experts, step, 0)
    send_first(experts - 1)
    if ORDER == 2:
        lax.fori_loop(0, experts, lambda e, c: (send_second(e), c)[1], 0)

    own = pltpu.make_async_copy(outbox.at[me], recv.at[me], own_sem.at[0])
    own.start()

    own_router.wait()
    for copy in router_rows:
        copy.wait()
    router_bands = []
    for j in range(1, groups):
        router_bands.append(
            pltpu.make_async_remote_copy(
                src_ref=band, dst_ref=band, send_sem=re_send.at[j], recv_sem=re_recv.at[j],
                device_id=(lax.rem(group + j, groups), me), device_id_type=MESH,
            )
        )
        router_bands[-1].start()
    for copy in router_bands:
        copy.wait()

    own.wait()
    for j in range(1, n):
        peer = lax.rem(me + j, n)
        pltpu.make_async_copy(outbox.at[peer], outbox.at[peer], send_sem.at[peer]).wait()
        pltpu.make_async_copy(recv.at[peer], recv.at[peer], recv_sem.at[peer]).wait()


def interleave_kernel(n, recv, gate, up):
    rows = recv.shape[-1]
    for d in range(n):
        gate[:, :, d * rows:(d + 1) * rows] = recv[d, :, 0]
        up[:, :, d * rows:(d + 1) * rows] = recv[d, :, 1]


def by_kernel(n, groups, master_gate, second_gate, master_up, second_up, part):
    experts, rows, width = master_gate.shape
    block = width // n
    columns = part.shape[0]
    anywhere = pl.BlockSpec(memory_space=pl.ANY)
    dma = pltpu.SemaphoreType.DMA
    recv, router = pl.pallas_call(
        functools.partial(exchange_kernel, n, groups),
        out_shape=(
            jax.ShapeDtypeStruct((n, experts, 2, block, rows), jnp.bfloat16),
            jax.ShapeDtypeStruct((groups * columns, n * rows), jnp.bfloat16),
        ),
        in_specs=[anywhere] * 5,
        out_specs=(anywhere, anywhere),
        scratch_shapes=[
            pltpu.VMEM((SLOTS, 2, rows, width), jnp.float32),
            pltpu.VMEM((SLOTS, 2, rows, width), jnp.bfloat16),
            pltpu.VMEM((n, experts, 2, block, rows), jnp.bfloat16),
            dma((SLOTS, 4)), dma((n,)), dma((n,)), dma((2,)),
            dma((n,)), dma((n,)), dma((groups,)), dma((groups,)),
        ],
        compiler_params=pltpu.CompilerParams(collective_id=0, has_side_effects=True),
    )(master_gate, second_gate, master_up, second_up, part)
    some = 2 if experts % 2 == 0 else 1
    whole = jax.ShapeDtypeStruct((experts, block, n * rows), jnp.bfloat16)
    gate, up = pl.pallas_call(
        functools.partial(interleave_kernel, n),
        grid=(experts // some,),
        out_shape=(whole, whole),
        in_specs=[pl.BlockSpec((n, some, 2, block, rows), lambda i: (0, i, 0, 0, 0))],
        out_specs=(pl.BlockSpec((some, block, n * rows), lambda i: (i, 0, 0)),) * 2,
    )(recv)
    return gate, up, router.T


def by_collectives(master_gate, second_gate, master_up, second_up, part):
    def moved(master, second):
        narrow = (master + second.astype(jnp.float32)).astype(jnp.bfloat16)
        sent = lax.all_to_all(narrow, "shard", split_axis=2, concat_axis=1, tiled=True)
        return jnp.transpose(sent, (0, 2, 1))

    bands = lax.all_gather(part.T, "shard", axis=0, tiled=True)
    router = lax.all_gather(bands, "expert", axis=1, tiled=True)
    return moved(master_gate, second_gate), moved(master_up, second_up), router


def per_device(n, groups, master_gate, second_gate, master_up, second_up, router_weight, router_gain):
    part = (router_weight * router_gain[:, None]).astype(jnp.bfloat16).T
    experts, rows, width = master_gate.shape
    fits = n >= 4 and n % 4 == 0 and groups > 1 and rows % 128 == 0 and width % (16 * n) == 0
    fits = fits and part.shape[0] % 16 == 0 and experts > SLOTS
    fits = fits and experts * rows * width * 4 + SLOTS * rows * width * 12 < 40 * 2**20
    if fits:
        return by_kernel(n, groups, master_gate, second_gate, master_up, second_up, part)
    return by_collectives(master_gate, second_gate, master_up, second_up, part)


def solution(mesh):
    placed = (
        P("expert", "shard", None),
        P("expert", "shard", None),
        P("expert", "shard", None),
        P("expert", "shard", None),
        P("shard", "expert"),
        P("shard"),
    )
    return jax.shard_map(
        functools.partial(per_device, mesh.shape["shard"], mesh.shape["expert"]),
        mesh=mesh,
        in_specs=placed,
        out_specs=(P("expert", "shard", None), P("expert", "shard", None), P()),
        check_vma=False,
    )
```

profile of v0, /device:TPU:14, one launch (start us, length us, event | category | flops | bytes accessed | tf_op | source)
XLA Modules:
  0.0 575.6 jit_solution(2706692291963753589)
XLA Ops:
  0.6 1.4 fusion.part
  2.0 548.6 %shard_map.85 = (bf16[8,32,2,96,256]{4,3,2,1,0:T(8,128)(2,1)}, bf16[128,2048]{1,0:T(8,128)(2,1)}) custom-call(f32[32,256,768]{2,1,0:T(8,128)} %mg.1, bf16[32,256,768]{2,1,0:T(8,128)(2,1)} %sg.1, f32[32,256,768]{2,1,0:T(8,128)} %mu.1, bf16[32,256,768]{2,1,0:T(8,128)(2,1)} %su.1, bf16[32,256]{1,0:T(8,128)(2,1)} %fusion.part), custom_call_target="tpu_custom_call" | custom-call | tf_op jit(solution)/shard_map/pallas_call | solution.py:165
  550.6 2.0 copy.9
  552.6 22.9 %shard_map.86 = (bf16[32,96,2048]{2,1,0:T(8,128)(2,1)}, bf16[32,96,2048]{2,1,0:T(8,128)(2,1)}) custom-call(bf16[8,32,2,96,256]{4,3,2,1,0:T(8,128)(2,1)} %get-tuple-element.7.recv), custom_call_target="tpu_custom_call" | custom-call | tf_op jit(solution)/shard_map/pallas_call | solution.py:184
where the time goes:
time: 581 us; the launch traced here: 576 us
  Pallas kernels  572 us (98%)
    pallas_call x1, Pallas kernels, by_kernel(): pl.pallas_call(functools.partial(exchange_kernel, n, groups), out_shape=(...  549 us
    pallas_call x1, Pallas kernels, by_kernel(): pl.pallas_call(functools.partial(interleave_kernel, n), grid=(experts //...  22.9 us

commit v1 on v0

v1 whole, which is shorter than its diff:
```python
import functools

import jax
import jax.numpy as jnp
from jax import lax
from jax.experimental import pallas as pl
from jax.experimental.pallas import tpu as pltpu
from jax.sharding import PartitionSpec as P

MESH = pl.DeviceIdType.MESH
SLOTS = 3
PIECES = 8
EXCHANGE_VMEM = 38 * 2**20
UNLOAD_VMEM = 4 * 2**20


def exchange_kernel(
    n, groups, mg, sg, mu, su, weight, gain, merged_all, own_block, router,
    wide, narrow, outbox, weight_in, gain_in, bands, turned_router,
    in_sem, send_sem, recv_sem, own_sem, rs_send, rs_recv, re_send, re_recv,
):
    experts, rows, _ = mg.shape
    block = outbox.shape[3]
    columns = weight.shape[0]
    me = lax.axis_index("shard")
    group = lax.axis_index("expert")

    def load(e):
        slot = lax.rem(e, SLOTS)
        return (
            pltpu.make_async_copy(mg.at[e], wide.at[slot, 0], in_sem.at[slot, 0]),
            pltpu.make_async_copy(sg.at[e], narrow.at[slot, 0], in_sem.at[slot, 1]),
            pltpu.make_async_copy(mu.at[e], wide.at[slot, 1], in_sem.at[slot, 2]),
            pltpu.make_async_copy(su.at[e], narrow.at[slot, 1], in_sem.at[slot, 3]),
        )

    barrier = pltpu.get_barrier_semaphore()
    for j in range(1, n):
        pl.semaphore_signal(barrier, inc=1, device_id=(group, lax.rem(me + j, n)), device_id_type=MESH)
    for j in range(1, groups):
        pl.semaphore_signal(barrier, inc=1, device_id=(lax.rem(group + j, groups), me), device_id_type=MESH)

    for e in range(SLOTS):
        for copy in load(e):
            copy.start()
    router_in = (
        pltpu.make_async_copy(weight, weight_in, own_sem.at[1]),
        pltpu.make_async_copy(gain, gain_in, own_sem.at[2]),
    )
    for copy in router_in:
        copy.start()
    for copy in router_in:
        copy.wait()
    band = bands.at[pl.ds(pl.multiple_of(group * columns, columns), columns)]
    cut = pl.ds(pl.multiple_of(me * rows, rows), rows)
    spot = band.at[:, cut]
    spot[...] = (weight_in[...] * gain_in[...]).astype(jnp.bfloat16)

    pl.semaphore_wait(barrier, n - 1 + groups - 1)

    half = n // 2
    lower = me < half
    near = [lax.rem(me + j, half) + jnp.where(lower, 0, half) for j in range(1, half)]
    far = [lax.rem(me + j, half) + jnp.where(lower, half, 0) for j in range(half)]

    def send(e):
        for peer in far + near:
            pltpu.make_async_remote_copy(
                src_ref=outbox.at[peer, e], dst_ref=merged_all.at[e, :, :, cut],
                send_sem=send_sem.at[peer], recv_sem=recv_sem.at[me],
                device_id=(group, peer), device_id_type=MESH,
            ).start()

    def step(e, _):
        slot = lax.rem(e, SLOTS)
        for copy in load(e):
            copy.wait()
        for which in range(2):
            merged = wide[slot, which] + narrow[slot, which].astype(jnp.float32)
            turned = merged.astype(jnp.bfloat16).T
            for d in range(n):
                outbox[d, e, which] = turned[d * block:(d + 1) * block]

        @pl.when(e + SLOTS < experts)
        def _():
            for copy in load(e + SLOTS):
                copy.start()

        @pl.when(e > 0)
        def _():
            send(e - 1)

        return 0

    step(0, 0)
    router_rows = []
    for j in range(1, n):
        router_rows.append(
            pltpu.make_async_remote_copy(
                src_ref=spot, dst_ref=spot, send_sem=rs_send.at[j], recv_sem=rs_recv.at[j],
                device_id=(group, lax.rem(me + j, n)), device_id_type=MESH,
            )
        )
        router_rows[-1].start()
    lax.fori_loop(1, experts, step, 0)
    send(experts - 1)

    own = pltpu.make_async_copy(outbox.at[me], own_block, own_sem.at[0])
    own.start()

    for copy in router_rows:
        copy.wait()
    router_bands = []
    for j in range(1, groups):
        router_bands.append(
            pltpu.make_async_remote_copy(
                src_ref=band, dst_ref=band, send_sem=re_send.at[j], recv_sem=re_recv.at[j],
                device_id=(lax.rem(group + j, groups), me), device_id_type=MESH,
            )
        )
        router_bands[-1].start()
    own.wait()
    own = pltpu.make_async_copy(own_block, merged_all.at[:, :, :, cut], own_sem.at[0])
    own.start()
    for copy in router_bands:
        copy.wait()
    for d in range(n):
        turned_router[d * rows:(d + 1) * rows] = bands[:, d * rows:(d + 1) * rows].T
    out_router = pltpu.make_async_copy(turned_router, router, own_sem.at[1])
    out_router.start()

    own.wait()
    out_router.wait()
    for j in range(1, n):
        peer = lax.rem(me + j, n)
        pltpu.make_async_copy(outbox.at[peer], outbox.at[peer], send_sem.at[peer]).wait()
        landed = merged_all.at[:, :, :, pl.ds(pl.multiple_of(peer * rows, rows), rows)]
        pltpu.make_async_copy(landed, landed, recv_sem.at[peer]).wait()


def unload_kernel(merged_all, router_in, gate, up, router, buffer, sem, router_sem):
    experts = merged_all.shape[0]
    pieces = sem.shape[1]
    some = experts // pieces
    fetch = pltpu.make_async_copy(router_in, buffer, router_sem.at[0])
    fetch.start()
    copies = []
    for i in range(pieces):
        part = pl.ds(i * some, some)
        for which, out in enumerate((gate, up)):
            copies.append(pltpu.make_async_copy(merged_all.at[part, which], out.at[part], sem.at[which, i]))
            copies[-1].start()
    fetch.wait()
    store = pltpu.make_async_copy(buffer, router, router_sem.at[1])
    store.start()
    for copy in copies:
        copy.wait()
    store.wait()


def by_kernel(n, groups, master_gate, second_gate, master_up, second_up, router_weight, router_gain):
    experts, rows, width = master_gate.shape
    block = width // n
    columns = router_weight.shape[1]
    anywhere = pl.BlockSpec(memory_space=pl.ANY)
    dma = pltpu.SemaphoreType.DMA
    bf16 = jnp.bfloat16
    merged_all, _, router = pl.pallas_call(
        functools.partial(exchange_kernel, n, groups),
        out_shape=(
            pltpu.VMEM((experts, 2, block, n * rows), bf16),
            pltpu.HBM((experts, 2, block, rows), bf16),
            pltpu.HBM((n * rows, groups * columns), bf16),
        ),
        in_specs=[anywhere] * 6,
        out_specs=(anywhere,) * 3,
        scratch_shapes=[
            pltpu.VMEM((SLOTS, 2, rows, width), jnp.float32),
            pltpu.VMEM((SLOTS, 2, rows, width), bf16),
            pltpu.VMEM((n, experts, 2, block, rows), bf16),
            pltpu.VMEM((columns, rows), jnp.float32),
            pltpu.VMEM((1, rows), jnp.float32),
            pltpu.VMEM((groups * columns, n * rows), bf16),
            pltpu.VMEM((n * rows, groups * columns), bf16),
            dma((SLOTS, 4)), dma((n,)), dma((n,)), dma((3,)),
            dma((n,)), dma((n,)), dma((groups,)), dma((groups,)),
        ],
        compiler_params=pltpu.CompilerParams(
            collective_id=0, has_side_effects=True, vmem_limit_bytes=EXCHANGE_VMEM
        ),
    )(master_gate, second_gate, master_up, second_up, router_weight.T, router_gain[None])
    pieces = PIECES if experts % PIECES == 0 else 1
    whole = jax.ShapeDtypeStruct((experts, block, n * rows), bf16)
    return pl.pallas_call(
        unload_kernel,
        out_shape=(whole, whole, jax.ShapeDtypeStruct(router.shape, bf16)),
        in_specs=[anywhere] * 2,
        out_specs=(anywhere,) * 3,
        scratch_shapes=[pltpu.VMEM(router.shape, bf16), dma((2, pieces)), dma((2,))],
        compiler_params=pltpu.CompilerParams(vmem_limit_bytes=UNLOAD_VMEM),
    )(pltpu.with_memory_space_constraint(merged_all, pltpu.VMEM), pltpu.with_memory_space_constraint(router, pltpu.HBM))


def by_collectives(master_gate, second_gate, master_up, second_up, part):
    def moved(master, second):
        narrow = (master + second.astype(jnp.float32)).astype(jnp.bfloat16)
        sent = lax.all_to_all(narrow, "shard", split_axis=2, concat_axis=1, tiled=True)
        return jnp.transpose(sent, (0, 2, 1))

    bands = lax.all_gather(part.T, "shard", axis=0, tiled=True)
    router = lax.all_gather(bands, "expert", axis=1, tiled=True)
    return moved(master_gate, second_gate), moved(master_up, second_up), router


def per_device(n, groups, master_gate, second_gate, master_up, second_up, router_weight, router_gain):
    experts, rows, width = master_gate.shape
    columns = router_weight.shape[1]
    fits = n >= 4 and n % 4 == 0 and groups > 1 and rows % 128 == 0 and width % (16 * n) == 0
    fits = fits and columns % 16 == 0 and experts > SLOTS
    fits = fits and experts * rows * width * 4 <= 24 * 2**20 and SLOTS * rows * width * 12 <= 7 * 2**20
    fits = fits and n * rows * groups * columns * 2 <= 2**20
    if fits:
        return by_kernel(n, groups, master_gate, second_gate, master_up, second_up, router_weight, router_gain)
    part = (router_weight * router_gain[:, None]).astype(jnp.bfloat16).T
    return by_collectives(master_gate, second_gate, master_up, second_up, part)


def solution(mesh):
    placed = (
        P("expert", "shard", None),
        P("expert", "shard", None),
        P("expert", "shard", None),
        P("expert", "shard", None),
        P("shard", "expert"),
        P("shard"),
    )
    return jax.shard_map(
        functools.partial(per_device, mesh.shape["shard"], mesh.shape["expert"]),
        mesh=mesh,
        in_specs=placed,
        out_specs=(P("expert", "shard", None), P("expert", "shard", None), P()),
        check_vma=False,
    )
```

time: 581 us -> 561 us (0.966)
  Pallas kernels: 572 us -> 557 us
    pallas_call x1, Pallas kernels: 22.9 us -> 8.65 us  [by_kernel(): pl.pallas_call(unload_kernel, out_shape=(whole, whole, jax.ShapeDtypeStru...]
where the time goes in v1:
time: 561 us; the launch traced here: 558 us
  Pallas kernels  557 us (99%)
    pallas_call x1, Pallas kernels, by_kernel(): pl.pallas_call(functools.partial(exchange_kernel, n, groups), out_shape=(...  549 us

profile of v1, /device:TPU:14, one launch (start us, length us, event | category | flops | bytes accessed | tf_op | source)
XLA Modules:
  0.0 558.0 jit_solution(7034676720200058013)
XLA Ops:
  0.6 548.7 %shard_map.85 = (bf16[32,2,96,2048]{3,2,1,0:T(8,128)(2,1)S(1)}, bf16[32,2,96,256]{3,2,1,0:T(8,128)(2,1)}, bf16[2048,128]{1,0:T(8,128)(2,1)}) custom-call(f32[32,256,768]{2,1,0:T(8,128)} %mg.1, bf16[32,256,768]{2,1,0:T(8,128)(2,1)} %sg.1, f32[32,256,768]{2,1,0:T(8,128)} %mu.1, bf16[32,256,768]{2,1,0:T(8,128)(2,1)} %su.1, f32[32,256]{1,0:T(8,128)} %bitcast.2, ...), custom_call_target="tpu_custom_call" | custom-call | tf_op jit(solution)/shard_map/pallas_call | solution.py:168
  549.3 8.7 %shard_map.86 = (bf16[32,96,2048]{2,1,0:T(8,128)(2,1)}, bf16[32,96,2048]{2,1,0:T(8,128)(2,1)}, bf16[2048,128]{1,0:T(8,128)(2,1)}) custom-call(bf16[32,2,96,2048]{3,2,1,0:T(8,128)(2,1)S(1)} %get-tuple-element.5.merged_all, bf16[2048,128]{1,0:T(8,128)(2,1)} %get-tuple-element.6.router_in), custom_call_target="tpu_custom_call" | custom-call | tf_op jit(solution)/shard_map/pallas_call | solution.py:194

commit v2 on v1

v2 whole, which is shorter than its diff:
```python
import functools

import jax
import jax.numpy as jnp
from jax import lax
from jax.experimental import pallas as pl
from jax.experimental.pallas import tpu as pltpu
from jax.sharding import PartitionSpec as P

MESH = pl.DeviceIdType.MESH
SLOTS = 3
LATE = (8, 4)
EXCHANGE_VMEM = 38 * 2**20
UNLOAD_VMEM = 4 * 2**20


def late_experts(group):
    return jnp.where(lax.rem(group, 2) == 0, LATE[0], LATE[1])


def exchange_kernel(n, groups, first, *refs):
    mg, sg, mu, su, *refs = refs
    if first:
        weight, gain, landed, own_block, router, *refs = refs
        wide, narrow, outbox, *refs = refs
        weight_in, gain_in, bands, turned_router, *refs = refs
        in_sem, send_sem, recv_sem, own_out, own_back, router_sem, rs_send, rs_recv, re_send, re_recv = refs
    else:
        _, landed, own_block, *refs = refs
        wide, narrow, outbox, in_sem, send_sem, recv_sem, own_out, own_back = refs
    experts, rows, _ = mg.shape
    block = outbox.shape[3]
    me = lax.axis_index("shard")
    group = lax.axis_index("expert")
    late = late_experts(group)
    base = 0 if first else experts - late
    count = experts - late if first else late

    barrier = pltpu.get_barrier_semaphore()
    for j in range(1, n):
        pl.semaphore_signal(barrier, inc=1, device_id=(group, lax.rem(me + j, n)), device_id_type=MESH)
    if first:
        for j in range(1, groups):
            pl.semaphore_signal(barrier, inc=1, device_id=(lax.rem(group + j, groups), me), device_id_type=MESH)

    def load(e):
        slot = lax.rem(e, SLOTS)
        return (
            pltpu.make_async_copy(mg.at[base + e], wide.at[slot, 0], in_sem.at[slot, 0]),
            pltpu.make_async_copy(sg.at[base + e], narrow.at[slot, 0], in_sem.at[slot, 1]),
            pltpu.make_async_copy(mu.at[base + e], wide.at[slot, 1], in_sem.at[slot, 2]),
            pltpu.make_async_copy(su.at[base + e], narrow.at[slot, 1], in_sem.at[slot, 3]),
        )

    for e in range(SLOTS):
        for copy in load(e):
            copy.start()
    cut = pl.ds(pl.multiple_of(me * rows, rows), rows)
    if first:
        router_in = (
            pltpu.make_async_copy(weight, weight_in, router_sem.at[0]),
            pltpu.make_async_copy(gain, gain_in, router_sem.at[1]),
        )
        for copy in router_in:
            copy.start()
        columns = weight.shape[0]
        band = bands.at[pl.ds(pl.multiple_of(group * columns, columns), columns)]
        spot = band.at[:, cut]

    half = n // 2
    lower = me < half
    near = [lax.rem(me + j, half) + jnp.where(lower, 0, half) for j in range(1, half)]
    far = [j + jnp.where(lower, half, 0) for j in range(half)]

    def remote(src, dst, e, peer):
        return pltpu.make_async_remote_copy(
            src_ref=src, dst_ref=dst, send_sem=send_sem.at[e], recv_sem=recv_sem.at[e],
            device_id=(group, peer), device_id_type=MESH,
        )

    def send(e):
        for peer in far + near:
            remote(outbox.at[peer, e], landed.at[e, :, :, cut], e, peer).start()

    def send_half(e, which):
        for peer in far + near:
            remote(outbox.at[peer, e, which], landed.at[e, which, :, cut], e, peer).start()

    def turn(e, which):
        slot = lax.rem(e, SLOTS)
        merged = wide[slot, which] + narrow[slot, which].astype(jnp.float32)
        turned = merged.astype(jnp.bfloat16).T
        for d in range(n):
            outbox[d, e, which] = turned[d * block:(d + 1) * block]

    def step(e, _):
        for copy in load(e):
            copy.wait()
        for which in range(2):
            turn(e, which)

        @pl.when(e + SLOTS < count)
        def _():
            for copy in load(e + SLOTS):
                copy.start()

        @pl.when(e > 1)
        def _():
            send(e - 1)

        return 0

    opening = load(0)
    for which in range(2):
        for copy in opening[2 * which:2 * which + 2]:
            copy.wait()
        turn(0, which)

    @pl.when(SLOTS < count)
    def _():
        for copy in load(SLOTS):
            copy.start()

    pl.semaphore_wait(barrier, n - 1 + (groups - 1 if first else 0))
    send_half(0, 0)
    if first:
        for copy in router_in:
            copy.wait()
        spot[...] = (weight_in[...] * gain_in[...]).astype(jnp.bfloat16)
    step(1, 0)
    send_half(0, 1)
    if first:
        router_rows = []
        for j in range(1, n):
            router_rows.append(
                pltpu.make_async_remote_copy(
                    src_ref=spot, dst_ref=spot, send_sem=rs_send.at[j], recv_sem=rs_recv.at[j],
                    device_id=(group, lax.rem(me + j, n)), device_id_type=MESH,
                )
            )
            router_rows[-1].start()
    lax.fori_loop(2, count, step, 0)
    send(count - 1)

    def leave(e):
        return pltpu.make_async_copy(outbox.at[me, e], own_block.at[e], own_out.at[e])

    def back(e):
        return pltpu.make_async_copy(own_block.at[e], landed.at[e, :, :, cut], own_back.at[e])

    def own_leave(e, _):
        leave(e).start()
        return 0

    def own_return(e, _):
        leave(e).wait()
        back(e).start()
        return 0

    lax.fori_loop(0, count, own_leave, 0)
    lax.fori_loop(0, count, own_return, 0)

    if first:
        for copy in router_rows:
            copy.wait()
        router_bands = []
        for j in range(1, groups):
            router_bands.append(
                pltpu.make_async_remote_copy(
                    src_ref=band, dst_ref=band, send_sem=re_send.at[j], recv_sem=re_recv.at[j],
                    device_id=(lax.rem(group + j, groups), me), device_id_type=MESH,
                )
            )
            router_bands[-1].start()
        for copy in router_bands:
            copy.wait()
        for d in range(n):
            turned_router[d * rows:(d + 1) * rows] = bands[:, d * rows:(d + 1) * rows].T
        out_router = pltpu.make_async_copy(turned_router, router, router_sem.at[0])
        out_router.start()
        out_router.wait()

    def finish(e, _):
        back(e).wait()
        gone = outbox.at[pl.ds(0, n - 1), e]
        pltpu.make_async_copy(gone, gone, send_sem.at[e]).wait()
        come = landed.at[e, :, :, pl.ds(0, (n - 1) * rows)]
        pltpu.make_async_copy(come, come, recv_sem.at[e]).wait()
        return 0

    lax.fori_loop(0, count, finish, 0)


def unload_kernel(first, *refs):
    if first:
        landed, router_in, gate, up, router, token, buffer, sem, router_sem = refs
    else:
        landed, _, _, gate, up, sem = refs
    experts = gate.shape[0]
    late = late_experts(lax.axis_index("expert"))
    base = 0 if first else experts - late
    count = experts - late if first else late

    def copies(e):
        return (
            pltpu.make_async_copy(landed.at[e, 0], gate.at[base + e], sem.at[0, e]),
            pltpu.make_async_copy(landed.at[e, 1], up.at[base + e], sem.at[1, e]),
        )

    def start(e, _):
        for copy in copies(e):
            copy.start()
        return 0

    def wait(e, _):
        for copy in copies(e):
            copy.wait()
        return 0

    if first:
        fetch = pltpu.make_async_copy(router_in, buffer, router_sem.at[0])
        fetch.start()
    lax.fori_loop(0, count, start, 0)
    if first:
        token[...] = jnp.zeros_like(token)
        fetch.wait()
        store = pltpu.make_async_copy(buffer, router, router_sem.at[1])
        store.start()
        store.wait()
    lax.fori_loop(0, count, wait, 0)


def by_kernel(n, groups, master_gate, second_gate, master_up, second_up, router_weight, router_gain):
    experts, rows, width = master_gate.shape
    block = width // n
    columns = router_weight.shape[1]
    anywhere = pl.BlockSpec(memory_space=pl.ANY)
    dma = pltpu.SemaphoreType.DMA
    bf16 = jnp.bfloat16
    whole = jax.ShapeDtypeStruct((experts, block, n * rows), bf16)
    router_shape = (n * rows, groups * columns)
    token_shape = jax.ShapeDtypeStruct((8, 128), jnp.float32)
    stay = functools.partial(pltpu.with_memory_space_constraint, memory_space=pltpu.HBM)
    masters = tuple(stay(x) for x in (master_gate, second_gate, master_up, second_up))

    def exchange(first, most, more, extra_out, extra_scratch, extra_sems):
        return pl.pallas_call(
            functools.partial(exchange_kernel, n, groups, first),
            out_shape=(
                pltpu.VMEM((most, 2, block, n * rows), bf16),
                pltpu.HBM((most, 2, block, rows), bf16),
                *extra_out,
            ),
            in_specs=[anywhere] * (4 + len(more)),
            out_specs=(anywhere,) * (2 + len(extra_out)),
            scratch_shapes=[
                pltpu.VMEM((SLOTS, 2, rows, width), jnp.float32),
                pltpu.VMEM((SLOTS, 2, rows, width), bf16),
                pltpu.VMEM((n, most, 2, block, rows), bf16),
                *extra_scratch,
                dma((SLOTS, 4)), dma((most,)), dma((most,)), dma((most,)), dma((most,)),
                *extra_sems,
            ],
            compiler_params=pltpu.CompilerParams(
                collective_id=0 if first else 1, has_side_effects=True, vmem_limit_bytes=EXCHANGE_VMEM
            ),
        )(*masters, *more)

    most = experts - min(LATE)
    landed, _, router = exchange(
        True, most, (stay(router_weight.T), stay(router_gain[None])),
        (pltpu.HBM(router_shape, bf16),),
        (
            pltpu.VMEM((columns, rows), jnp.float32),
            pltpu.VMEM((1, rows), jnp.float32),
            pltpu.VMEM((groups * columns, n * rows), bf16),
            pltpu.VMEM(router_shape, bf16),
        ),
        (dma((2,)), dma((n,)), dma((n,)), dma((groups,)), dma((groups,))),
    )
    gate, up, router, token = pl.pallas_call(
        functools.partial(unload_kernel, True),
        out_shape=(whole, whole, jax.ShapeDtypeStruct(router_shape, bf16), token_shape),
        in_specs=[anywhere] * 2,
        out_specs=(anywhere,) * 3 + (pl.BlockSpec(memory_space=pltpu.VMEM),),
        scratch_shapes=[pltpu.VMEM(router_shape, bf16), dma((2, most)), dma((2,))],
        compiler_params=pltpu.CompilerParams(vmem_limit_bytes=UNLOAD_VMEM),
    )(pltpu.with_memory_space_constraint(landed, pltpu.VMEM), stay(router))
    landed, _ = exchange(False, max(LATE), (token,), (), (), ())
    gate, up = pl.pallas_call(
        functools.partial(unload_kernel, False),
        out_shape=(whole, whole),
        in_specs=[anywhere] * 3,
        out_specs=(anywhere,) * 2,
        scratch_shapes=[dma((2, max(LATE)))],
        input_output_aliases={1: 0, 2: 1},
        compiler_params=pltpu.CompilerParams(vmem_limit_bytes=UNLOAD_VMEM),
    )(pltpu.with_memory_space_constraint(landed, pltpu.VMEM), stay(gate), stay(up))
    return gate, up, router


def by_collectives(master_gate, second_gate, master_up, second_up, part):
    def moved(master, second):
        narrow = (master + second.astype(jnp.float32)).astype(jnp.bfloat16)
        sent = lax.all_to_all(narrow, "shard", split_axis=2, concat_axis=1, tiled=True)
        return jnp.transpose(sent, (0, 2, 1))

    bands = lax.all_gather(part.T, "shard", axis=0, tiled=True)
    router = lax.all_gather(bands, "expert", axis=1, tiled=True)
    return moved(master_gate, second_gate), moved(master_up, second_up), router


def per_device(n, groups, master_gate, second_gate, master_up, second_up, router_weight, router_gain):
    experts, rows, width = master_gate.shape
    columns = router_weight.shape[1]
    fits = n >= 4 and n % 4 == 0 and groups > 1 and rows % 128 == 0 and width % (16 * n) == 0
    fits = fits and columns % 16 == 0 and min(LATE) >= SLOTS and experts - max(LATE) > SLOTS
    fits = fits and experts * rows * width * 4 <= 24 * 2**20 and SLOTS * rows * width * 12 <= 7 * 2**20
    fits = fits and n * rows * groups * columns * 2 <= 2**20
    if fits:
        return by_kernel(n, groups, master_gate, second_gate, master_up, second_up, router_weight, router_gain)
    part = (router_weight * router_gain[:, None]).astype(jnp.bfloat16).T
    return by_collectives(master_gate, second_gate, master_up, second_up, part)


def solution(mesh):
    placed = (
        P("expert", "shard", None),
        P("expert", "shard", None),
        P("expert", "shard", None),
        P("expert", "shard", None),
        P("shard", "expert"),
        P("shard"),
    )
    return jax.shard_map(
        functools.partial(per_device, mesh.shape["shard"], mesh.shape["expert"]),
        mesh=mesh,
        in_specs=placed,
        out_specs=(P("expert", "shard", None), P("expert", "shard", None), P()),
        check_vma=False,
    )
```

time: 561 us -> 551 us (0.982)
  Pallas kernels: 557 us -> 550 us
    pallas_call x2 -> x4, Pallas kernels: 557 us -> 550 us  [the longest x2 540 us: exchange(): pl.pallas_call(functools.partial(exchange_kernel, n, groups, first), out_...]
where the time goes in v2:
time: 551 us
  Pallas kernels  550 us (100%)
    pallas_call x2, Pallas kernels, exchange(): pl.pallas_call(functools.partial(exchange_kernel, n, groups, first), out_...  540 us

profile of v2, /device:TPU:14, one launch (start us, length us, event | category | flops | bytes accessed | tf_op | source)
XLA Modules:
  0.0 551.1 jit_solution(10464196235713169657)
XLA Ops:
  0.6 431.1 %shard_map.85 = (bf16[28,2,96,2048]{3,2,1,0:T(8,128)(2,1)S(1)}, bf16[28,2,96,256]{3,2,1,0:T(8,128)(2,1)}, bf16[2048,128]{1,0:T(8,128)(2,1)}) custom-call(f32[32,256,768]{2,1,0:T(8,128)} %refs_0_.3, bf16[32,256,768]{2,1,0:T(8,128)(2,1)} %refs_1_.3, f32[32,256,768]{2,1,0:T(8,128)} %refs_2_.3, bf16[32,256,768]{2,1,0:T(8,128)(2,1)} %refs_3_.3, ...), custom_call_target="tpu_custom_call" | custom-call | tf_op jit(solution)/shard_map/pallas_call | solution.py:247
  431.8 7.3 %shard_map.86 = (bf16[32,96,2048]{2,1,0:T(8,128)(2,1)}, bf16[32,96,2048]{2,1,0:T(8,128)(2,1)}, bf16[2048,128]{1,0:T(8,128)(2,1)}, f32[8,128]{1,0:T(8,128)S(1)}) custom-call(bf16[28,2,96,2048]{3,2,1,0:T(8,128)(2,1)S(1)} %get-tuple-element.12.refs_0_, bf16[2048,128]{1,0:T(8,128)(2,1)} %get-tuple-element.13.refs_1_), custom_call_target="tpu_custom_call" | custom-call | tf_op jit(solution)/shard_map/pallas_call | solution.py:281
  439.0 109.3 %shard_map.87 = (bf16[8,2,96,2048]{3,2,1,0:T(8,128)(2,1)S(1)}, bf16[8,2,96,256]{3,2,1,0:T(8,128)(2,1)}) custom-call(f32[32,256,768]{2,1,0:T(8,128)} %refs_0_.3, bf16[32,256,768]{2,1,0:T(8,128)(2,1)} %refs_1_.3, f32[32,256,768]{2,1,0:T(8,128)} %refs_2_.3, bf16[32,256,768]{2,1,0:T(8,128)(2,1)} %refs_3_.3, f32[8,128]{1,0:T(8,128)S(1)} %get-tuple-element.14.refs_4_), custom_call_target="tpu_custom_call" | custom-call | tf_op jit(solution)/shard_map/pallas_call | solution.py:247
  548.3 2.8 shard_map.88

commit v3 on v2

--- a/solution.py
+++ b/solution.py
@@ -9,7 +9,7 @@
 
 MESH = pl.DeviceIdType.MESH
 SLOTS = 3
-LATE = (8, 4)
+LATE = (6, 2)
 EXCHANGE_VMEM = 38 * 2**20
 UNLOAD_VMEM = 4 * 2**20
 
@@ -24,11 +24,12 @@
         weight, gain, landed, own_block, router, *refs = refs
         wide, narrow, outbox, *refs = refs
         weight_in, gain_in, bands, turned_router, *refs = refs
-        in_sem, send_sem, recv_sem, own_out, own_back, router_sem, rs_send, rs_recv, re_send, re_recv = refs
+        in_sem, send_sem, recv_sem, own_out, own_back, router_sem, rs_send, rs_recv, rl_send, rl_recv, re_send, re_recv = refs
     else:
         _, landed, own_block, *refs = refs
         wide, narrow, outbox, in_sem, send_sem, recv_sem, own_out, own_back = refs
     experts, rows, _ = mg.shape
+    slots = wide.shape[0]
     block = outbox.shape[3]
     me = lax.axis_index("shard")
     group = lax.axis_index("expert")
@@ -44,7 +45,7 @@
             pl.semaphore_signal(barrier, inc=1, device_id=(lax.rem(group + j, groups), me), device_id_type=MESH)
 
     def load(e):
-        slot = lax.rem(e, SLOTS)
+        slot = lax.rem(e, slots)
         return (
             pltpu.make_async_copy(mg.at[base + e], wide.at[slot, 0], in_sem.at[slot, 0]),
             pltpu.make_async_copy(sg.at[base + e], narrow.at[slot, 0], in_sem.at[slot, 1]),
@@ -52,7 +53,7 @@
             pltpu.make_async_copy(su.at[base + e], narrow.at[slot, 1], in_sem.at[slot, 3]),
         )
 
-    for e in range(SLOTS):
+    for e in range(slots):
         for copy in load(e):
             copy.start()
     cut = pl.ds(pl.multiple_of(me * rows, rows), rows)
@@ -87,7 +88,7 @@
             remote(outbox.at[peer, e, which], landed.at[e, which, :, cut], e, peer).start()
 
     def turn(e, which):
-        slot = lax.rem(e, SLOTS)
+        slot = lax.rem(e, slots)
         merged = wide[slot, which] + narrow[slot, which].astype(jnp.float32)
         turned = merged.astype(jnp.bfloat16).T
         for d in range(n):
@@ -99,9 +100,9 @@
         for which in range(2):
             turn(e, which)
 
-        @pl.when(e + SLOTS < count)
+        @pl.when(e + slots < count)
         def _():
-            for copy in load(e + SLOTS):
+            for copy in load(e + slots):
                 copy.start()
 
         @pl.when(e > 1)
@@ -116,9 +117,9 @@
             copy.wait()
         turn(0, which)
 
-    @pl.when(SLOTS < count)
+    @pl.when(slots < count)
     def _():
-        for copy in load(SLOTS):
+        for copy in load(slots):
             copy.start()
 
     pl.semaphore_wait(barrier, n - 1 + (groups - 1 if first else 0))
@@ -130,16 +131,28 @@
     step(1, 0)
     send_half(0, 1)
     if first:
+        partner = lax.rem(me + half, n)
         router_rows = []
-        for j in range(1, n):
+        for j, peer in enumerate([partner] + near):
             router_rows.append(
                 pltpu.make_async_remote_copy(
                     src_ref=spot, dst_ref=spot, send_sem=rs_send.at[j], recv_sem=rs_recv.at[j],
-                    device_id=(group, lax.rem(me + j, n)), device_id_type=MESH,
+                    device_id=(group, peer), device_id_type=MESH,
                 )
             )
             router_rows[-1].start()
-    lax.fori_loop(2, count, step, 0)
+        lax.fori_loop(2, SLOTS + 1, step, 0)
+        router_rows[0].wait()
+        passed = band.at[:, pl.ds(pl.multiple_of(partner * rows, rows), rows)]
+        for j, peer in enumerate(near):
+            router_rows.append(
+                pltpu.make_async_remote_copy(
+                    src_ref=passed, dst_ref=passed, send_sem=rl_send.at[j], recv_sem=rl_recv.at[j],
+                    device_id=(group, peer), device_id_type=MESH,
+                )
+            )
+            router_rows[-1].start()
+    lax.fori_loop(SLOTS + 1 if first else 2, count, step, 0)
     send(count - 1)
 
     def leave(e):
@@ -161,7 +174,7 @@
     lax.fori_loop(0, count, own_return, 0)
 
     if first:
-        for copy in router_rows:
+        for copy in router_rows[1:]:
             copy.wait()
         router_bands = []
         for j in range(1, groups):
@@ -244,6 +257,7 @@
     masters = tuple(stay(x) for x in (master_gate, second_gate, master_up, second_up))
 
     def exchange(first, most, more, extra_out, extra_scratch, extra_sems):
+        slots = SLOTS if first else min(SLOTS, *LATE)
         return pl.pallas_call(
             functools.partial(exchange_kernel, n, groups, first),
             out_shape=(
@@ -254,11 +268,11 @@
             in_specs=[anywhere] * (4 + len(more)),
             out_specs=(anywhere,) * (2 + len(extra_out)),
             scratch_shapes=[
-                pltpu.VMEM((SLOTS, 2, rows, width), jnp.float32),
-                pltpu.VMEM((SLOTS, 2, rows, width), bf16),
+                pltpu.VMEM((slots, 2, rows, width), jnp.float32),
+                pltpu.VMEM((slots, 2, rows, width), bf16),
                 pltpu.VMEM((n, most, 2, block, rows), bf16),
                 *extra_scratch,
-                dma((SLOTS, 4)), dma((most,)), dma((most,)), dma((most,)), dma((most,)),
+                dma((slots, 4)), dma((most,)), dma((most,)), dma((most,)), dma((most,)),
                 *extra_sems,
             ],
             compiler_params=pltpu.CompilerParams(
@@ -276,7 +290,7 @@
             pltpu.VMEM((groups * columns, n * rows), bf16),
             pltpu.VMEM(router_shape, bf16),
         ),
-        (dma((2,)), dma((n,)), dma((n,)), dma((groups,)), dma((groups,))),
+        (dma((2,)), *[dma((n // 2,))] * 4, dma((groups,)), dma((groups,))),
     )
     gate, up, router, token = pl.pallas_call(
         functools.partial(unload_kernel, True),
@@ -314,7 +328,7 @@
     experts, rows, width = master_gate.shape
     columns = router_weight.shape[1]
     fits = n >= 4 and n % 4 == 0 and groups > 1 and rows % 128 == 0 and width % (16 * n) == 0
-    fits = fits and columns % 16 == 0 and min(LATE) >= SLOTS and experts - max(LATE) > SLOTS
+    fits = fits and columns % 16 == 0 and min(LATE) >= 2 and experts - max(LATE) > SLOTS
     fits = fits and experts * rows * width * 4 <= 24 * 2**20 and SLOTS * rows * width * 12 <= 7 * 2**20
     fits = fits and n * rows * groups * columns * 2 <= 2**20
     if fits:

time: 551 us -> 549 us (level)
  no operation moved by 1% of the time
where the time goes in v3:
time: 549 us
  Pallas kernels  548 us (100%)
    pallas_call x2, Pallas kernels, exchange(): pl.pallas_call(functools.partial(exchange_kernel, n, groups, first), out_...  538 us

profile of v3, /device:TPU:14, one launch (start us, length us, event | category | flops | bytes accessed | tf_op | source)
XLA Modules:
  0.0 548.6 jit_solution(13270867871222217195)
XLA Ops:
  0.6 463.1 %shard_map.85 = (bf16[30,2,96,2048]{3,2,1,0:T(8,128)(2,1)S(1)}, bf16[30,2,96,256]{3,2,1,0:T(8,128)(2,1)}, bf16[2048,128]{1,0:T(8,128)(2,1)}) custom-call(f32[32,256,768]{2,1,0:T(8,128)} %refs_0_.3, bf16[32,256,768]{2,1,0:T(8,128)(2,1)} %refs_1_.3, f32[32,256,768]{2,1,0:T(8,128)} %refs_2_.3, bf16[32,256,768]{2,1,0:T(8,128)(2,1)} %refs_3_.3, ...), custom_call_target="tpu_custom_call" | custom-call | tf_op jit(solution)/shard_map/pallas_call | solution.py:261
  463.7 7.8 %shard_map.86 = (bf16[32,96,2048]{2,1,0:T(8,128)(2,1)}, bf16[32,96,2048]{2,1,0:T(8,128)(2,1)}, bf16[2048,128]{1,0:T(8,128)(2,1)}, f32[8,128]{1,0:T(8,128)S(1)}) custom-call(bf16[30,2,96,2048]{3,2,1,0:T(8,128)(2,1)S(1)} %get-tuple-element.12.refs_0_, bf16[2048,128]{1,0:T(8,128)(2,1)} %get-tuple-element.13.refs_1_), custom_call_target="tpu_custom_call" | custom-call | tf_op jit(solution)/shard_map/pallas_call | solution.py:295
  471.5 74.8 %shard_map.87 = (bf16[6,2,96,2048]{3,2,1,0:T(8,128)(2,1)S(1)}, bf16[6,2,96,256]{3,2,1,0:T(8,128)(2,1)}) custom-call(f32[32,256,768]{2,1,0:T(8,128)} %refs_0_.3, bf16[32,256,768]{2,1,0:T(8,128)(2,1)} %refs_1_.3, f32[32,256,768]{2,1,0:T(8,128)} %refs_2_.3, bf16[32,256,768]{2,1,0:T(8,128)(2,1)} %refs_3_.3, f32[8,128]{1,0:T(8,128)S(1)} %get-tuple-element.14.refs_4_), custom_call_target="tpu_custom_call" | custom-call | tf_op jit(solution)/shard_map/pallas_call | solution.py:261
  546.3 2.3 shard_map.88

commit v4 on v2

v4 whole, which is shorter than its diff:
```python
import functools

import jax
import jax.numpy as jnp
from jax import lax
from jax.experimental import pallas as pl
from jax.experimental.pallas import tpu as pltpu
from jax.sharding import PartitionSpec as P

MESH = pl.DeviceIdType.MESH
SLOTS = 3
LATE = ((6, 2), (2, 0))
EXCHANGE_VMEM = 38 * 2**20
UNLOAD_VMEM = 4 * 2**20


def span(group, experts, phase):
    later = [jnp.where(lax.rem(group, 2) == 0, even, odd) for even, odd in LATE]
    if phase == 0:
        return 0, experts - sum(later)
    return experts - sum(later[phase - 1:]), later[phase - 1]


def exchange_kernel(n, groups, phase, *refs):
    first = phase == 0
    mg, sg, mu, su, *refs = refs
    if first:
        weight, gain, landed, own_block, router, *refs = refs
        wide, narrow, outbox, *refs = refs
        weight_in, gain_in, bands, turned_router, *refs = refs
        in_sem, send_sem, recv_sem, own_out, own_back, router_sem, rs_send, rs_recv, rl_send, rl_recv, re_send, re_recv = refs
    else:
        _, landed, own_block, *refs = refs
        wide, narrow, outbox, in_sem, send_sem, recv_sem, own_out, own_back = refs
    experts, rows, _ = mg.shape
    slots = wide.shape[0]
    block = outbox.shape[3]
    me = lax.axis_index("shard")
    group = lax.axis_index("expert")
    base, count = span(group, experts, phase)

    def body():
        barrier = pltpu.get_barrier_semaphore()
        for j in range(1, n):
            pl.semaphore_signal(barrier, inc=1, device_id=(group, lax.rem(me + j, n)), device_id_type=MESH)
        if first:
            for j in range(1, groups):
                pl.semaphore_signal(barrier, inc=1, device_id=(lax.rem(group + j, groups), me), device_id_type=MESH)

        def load(e):
            slot = lax.rem(e, slots)
            return (
                pltpu.make_async_copy(mg.at[base + e], wide.at[slot, 0], in_sem.at[slot, 0]),
                pltpu.make_async_copy(sg.at[base + e], narrow.at[slot, 0], in_sem.at[slot, 1]),
                pltpu.make_async_copy(mu.at[base + e], wide.at[slot, 1], in_sem.at[slot, 2]),
                pltpu.make_async_copy(su.at[base + e], narrow.at[slot, 1], in_sem.at[slot, 3]),
            )

        for e in range(slots):
            for copy in load(e):
                copy.start()
        cut = pl.ds(pl.multiple_of(me * rows, rows), rows)
        if first:
            router_in = (
                pltpu.make_async_copy(weight, weight_in, router_sem.at[0]),
                pltpu.make_async_copy(gain, gain_in, router_sem.at[1]),
            )
            for copy in router_in:
                copy.start()
            columns = weight.shape[0]
            band = bands.at[pl.ds(pl.multiple_of(group * columns, columns), columns)]
            spot = band.at[:, cut]

        half = n // 2
        lower = me < half
        near = [lax.rem(me + j, half) + jnp.where(lower, 0, half) for j in range(1, half)]
        far = [j + jnp.where(lower, half, 0) for j in range(half)]

        def remote(src, dst, e, peer):
            return pltpu.make_async_remote_copy(
                src_ref=src, dst_ref=dst, send_sem=send_sem.at[e], recv_sem=recv_sem.at[e],
                device_id=(group, peer), device_id_type=MESH,
            )

        def send(e):
            for peer in far + near:
                remote(outbox.at[peer, e], landed.at[e, :, :, cut], e, peer).start()

        def send_half(e, which):
            for peer in far + near:
                remote(outbox.at[peer, e, which], landed.at[e, which, :, cut], e, peer).start()

        def turn(e, which):
            slot = lax.rem(e, slots)
            merged = wide[slot, which] + narrow[slot, which].astype(jnp.float32)
            turned = merged.astype(jnp.bfloat16).T
            for d in range(n):
                outbox[d, e, which] = turned[d * block:(d + 1) * block]

        def step(e, _):
            for copy in load(e):
                copy.wait()
            for which in range(2):
                turn(e, which)

            @pl.when(e + slots < count)
            def _():
                for copy in load(e + slots):
                    copy.start()

            @pl.when(e > 1)
            def _():
                send(e - 1)

            return 0

        opening = load(0)
        for which in range(2):
            for copy in opening[2 * which:2 * which + 2]:
                copy.wait()
            turn(0, which)

        @pl.when(slots < count)
        def _():
            for copy in load(slots):
                copy.start()

        pl.semaphore_wait(barrier, n - 1 + (groups - 1 if first else 0))
        send_half(0, 0)
        if first:
            for copy in router_in:
                copy.wait()
            spot[...] = (weight_in[...] * gain_in[...]).astype(jnp.bfloat16)
        step(1, 0)
        send_half(0, 1)
        if first:
            partner = lax.rem(me + half, n)
            router_rows = []
            for j, peer in enumerate([partner] + near):
                router_rows.append(
                    pltpu.make_async_remote_copy(
                        src_ref=spot, dst_ref=spot, send_sem=rs_send.at[j], recv_sem=rs_recv.at[j],
                        device_id=(group, peer), device_id_type=MESH,
                    )
                )
                router_rows[-1].start()
            lax.fori_loop(2, SLOTS + 1, step, 0)
            router_rows[0].wait()
            passed = band.at[:, pl.ds(pl.multiple_of(partner * rows, rows), rows)]
            for j, peer in enumerate(near):
                router_rows.append(
                    pltpu.make_async_remote_copy(
                        src_ref=passed, dst_ref=passed, send_sem=rl_send.at[j], recv_sem=rl_recv.at[j],
                        device_id=(group, peer), device_id_type=MESH,
                    )
                )
                router_rows[-1].start()
        lax.fori_loop(SLOTS + 1 if first else 2, count, step, 0)
        send(count - 1)

        def leave(e):
            return pltpu.make_async_copy(outbox.at[me, e], own_block.at[e], own_out.at[e])

        def back(e):
            return pltpu.make_async_copy(own_block.at[e], landed.at[e, :, :, cut], own_back.at[e])

        def own_leave(e, _):
            leave(e).start()
            return 0

        def own_return(e, _):
            leave(e).wait()
            back(e).start()
            return 0

        lax.fori_loop(0, count, own_leave, 0)
        lax.fori_loop(0, count, own_return, 0)

        if first:
            for copy in router_rows[1:]:
                copy.wait()
            router_bands = []
            for j in range(1, groups):
                router_bands.append(
                    pltpu.make_async_remote_copy(
                        src_ref=band, dst_ref=band, send_sem=re_send.at[j], recv_sem=re_recv.at[j],
                        device_id=(lax.rem(group + j, groups), me), device_id_type=MESH,
                    )
                )
                router_bands[-1].start()
            for copy in router_bands:
                copy.wait()
            for d in range(n):
                turned_router[d * rows:(d + 1) * rows] = bands[:, d * rows:(d + 1) * rows].T
            out_router = pltpu.make_async_copy(turned_router, router, router_sem.at[0])
            out_router.start()
            out_router.wait()

        def finish(e, _):
            back(e).wait()
            gone = outbox.at[pl.ds(0, n - 1), e]
            pltpu.make_async_copy(gone, gone, send_sem.at[e]).wait()
            come = landed.at[e, :, :, pl.ds(0, (n - 1) * rows)]
            pltpu.make_async_copy(come, come, recv_sem.at[e]).wait()
            return 0

        lax.fori_loop(0, count, finish, 0)

    if first or min(LATE[phase - 1]) > 0:
        body()
    else:
        pl.when(count > 0)(body)


def unload_kernel(phase, *refs):
    first = phase == 0
    last = phase == len(LATE)
    if first:
        landed, router_in, gate, up, token, router, buffer, sem, router_sem = refs
    elif last:
        landed, _, _, gate, up, sem = refs
    else:
        landed, _, _, gate, up, token, sem = refs
    base, count = span(lax.axis_index("expert"), gate.shape[0], phase)

    def copies(e):
        return (
            pltpu.make_async_copy(landed.at[e, 0], gate.at[base + e], sem.at[0, e]),
            pltpu.make_async_copy(landed.at[e, 1], up.at[base + e], sem.at[1, e]),
        )

    def start(e, _):
        for copy in copies(e):
            copy.start()
        return 0

    def wait(e, _):
        for copy in copies(e):
            copy.wait()
        return 0

    if first:
        fetch = pltpu.make_async_copy(router_in, buffer, router_sem.at[0])
        fetch.start()
    lax.fori_loop(0, count, start, 0)
    if not last:
        token[...] = jnp.zeros_like(token)
    if first:
        fetch.wait()
        store = pltpu.make_async_copy(buffer, router, router_sem.at[1])
        store.start()
        store.wait()
    lax.fori_loop(0, count, wait, 0)


def by_kernel(n, groups, master_gate, second_gate, master_up, second_up, router_weight, router_gain):
    experts, rows, width = master_gate.shape
    block = width // n
    columns = router_weight.shape[1]
    anywhere = pl.BlockSpec(memory_space=pl.ANY)
    dma = pltpu.SemaphoreType.DMA
    bf16 = jnp.bfloat16
    whole = jax.ShapeDtypeStruct((experts, block, n * rows), bf16)
    router_shape = (n * rows, groups * columns)
    token_shape = jax.ShapeDtypeStruct((8, 128), jnp.float32)
    stay = functools.partial(pltpu.with_memory_space_constraint, memory_space=pltpu.HBM)
    masters = tuple(stay(x) for x in (master_gate, second_gate, master_up, second_up))

    def exchange(phase, most, more, extra_out, extra_scratch, extra_sems):
        slots = min(SLOTS, *(x for x in LATE[phase - 1] if x)) if phase else SLOTS
        return pl.pallas_call(
            functools.partial(exchange_kernel, n, groups, phase),
            out_shape=(
                pltpu.VMEM((most, 2, block, n * rows), bf16),
                pltpu.HBM((most, 2, block, rows), bf16),
                *extra_out,
            ),
            in_specs=[anywhere] * (4 + len(more)),
            out_specs=(anywhere,) * (2 + len(extra_out)),
            scratch_shapes=[
                pltpu.VMEM((slots, 2, rows, width), jnp.float32),
                pltpu.VMEM((slots, 2, rows, width), bf16),
                pltpu.VMEM((n, most, 2, block, rows), bf16),
                *extra_scratch,
                dma((slots, 4)), dma((most,)), dma((most,)), dma((most,)), dma((most,)),
                *extra_sems,
            ],
            compiler_params=pltpu.CompilerParams(
                collective_id=phase, has_side_effects=True, vmem_limit_bytes=EXCHANGE_VMEM
            ),
        )(*masters, *more)

    most = experts - min(sum(x) for x in zip(*LATE))
    landed, _, router = exchange(
        0, most, (stay(router_weight.T), stay(router_gain[None])),
        (pltpu.HBM(router_shape, bf16),),
        (
            pltpu.VMEM((columns, rows), jnp.float32),
            pltpu.VMEM((1, rows), jnp.float32),
            pltpu.VMEM((groups * columns, n * rows), bf16),
            pltpu.VMEM(router_shape, bf16),
        ),
        (dma((2,)), *[dma((n // 2,))] * 4, dma((groups,)), dma((groups,))),
    )
    in_vmem = pl.BlockSpec(memory_space=pltpu.VMEM)
    unload_params = pltpu.CompilerParams(vmem_limit_bytes=UNLOAD_VMEM)
    gate, up, token, router = pl.pallas_call(
        functools.partial(unload_kernel, 0),
        out_shape=(whole, whole, token_shape, jax.ShapeDtypeStruct(router_shape, bf16)),
        in_specs=[anywhere] * 2,
        out_specs=(anywhere, anywhere, in_vmem, anywhere),
        scratch_shapes=[pltpu.VMEM(router_shape, bf16), dma((2, most)), dma((2,))],
        compiler_params=unload_params,
    )(pltpu.with_memory_space_constraint(landed, pltpu.VMEM), stay(router))
    for phase, late in enumerate(LATE, 1):
        last = phase == len(LATE)
        landed, _ = exchange(phase, max(late), (token,), (), (), ())
        out = pl.pallas_call(
            functools.partial(unload_kernel, phase),
            out_shape=(whole, whole) if last else (whole, whole, token_shape),
            in_specs=[anywhere] * 3,
            out_specs=(anywhere, anywhere) if last else (anywhere, anywhere, in_vmem),
            scratch_shapes=[dma((2, max(late)))],
            input_output_aliases={1: 0, 2: 1},
            compiler_params=unload_params,
        )(pltpu.with_memory_space_constraint(landed, pltpu.VMEM), stay(gate), stay(up))
        gate, up, token = out if not last else (*out, None)
    return gate, up, router


def by_collectives(master_gate, second_gate, master_up, second_up, part):
    def moved(master, second):
        narrow = (master + second.astype(jnp.float32)).astype(jnp.bfloat16)
        sent = lax.all_to_all(narrow, "shard", split_axis=2, concat_axis=1, tiled=True)
        return jnp.transpose(sent, (0, 2, 1))

    bands = lax.all_gather(part.T, "shard", axis=0, tiled=True)
    router = lax.all_gather(bands, "expert", axis=1, tiled=True)
    return moved(master_gate, second_gate), moved(master_up, second_up), router


def per_device(n, groups, master_gate, second_gate, master_up, second_up, router_weight, router_gain):
    experts, rows, width = master_gate.shape
    columns = router_weight.shape[1]
    fits = n >= 4 and n % 4 == 0 and groups > 1 and rows % 128 == 0 and width % (16 * n) == 0
    fits = fits and columns % 16 == 0 and experts - max(sum(x) for x in zip(*LATE)) > SLOTS
    fits = fits and experts * rows * width * 4 <= 24 * 2**20 and SLOTS * rows * width * 12 <= 7 * 2**20
    fits = fits and n * rows * groups * columns * 2 <= 2**20
    if fits:
        return by_kernel(n, groups, master_gate, second_gate, master_up, second_up, router_weight, router_gain)
    part = (router_weight * router_gain[:, None]).astype(jnp.bfloat16).T
    return by_collectives(master_gate, second_gate, master_up, second_up, part)


def solution(mesh):
    placed = (
        P("expert", "shard", None),
        P("expert", "shard", None),
        P("expert", "shard", None),
        P("expert", "shard", None),
        P("shard", "expert"),
        P("shard"),
    )
    return jax.shard_map(
        functools.partial(per_device, mesh.shape["shard"], mesh.shape["expert"]),
        mesh=mesh,
        in_specs=placed,
        out_specs=(P("expert", "shard", None), P("expert", "shard", None), P()),
        check_vma=False,
    )
```

time: 551 us -> 548 us (level)
    pallas_call x4 -> x6, Pallas kernels: 550 us -> 547 us  [the longest x3 536 us: exchange(): pl.pallas_call(functools.partial(exchange_kernel, n, groups, phase), out_...]
where the time goes in v4:
time: 548 us; the launch traced here: 547 us
  Pallas kernels  547 us (100%)
    pallas_call x3, Pallas kernels, exchange(): pl.pallas_call(functools.partial(exchange_kernel, n, groups, phase), out_...  536 us

profile of v4, /device:TPU:14, one launch (start us, length us, event | category | flops | bytes accessed | tf_op | source)
XLA Modules:
  0.0 547.4 jit_solution(13007425692174029586)
XLA Ops:
  0.6 437.8 %shard_map.85 = (bf16[30,2,96,2048]{3,2,1,0:T(8,128)(2,1)S(1)}, bf16[30,2,96,256]{3,2,1,0:T(8,128)(2,1)}, bf16[2048,128]{1,0:T(8,128)(2,1)}) custom-call(f32[32,256,768]{2,1,0:T(8,128)} %refs_0_.5, bf16[32,256,768]{2,1,0:T(8,128)(2,1)} %refs_1_.5, f32[32,256,768]{2,1,0:T(8,128)} %refs_2_.5, bf16[32,256,768]{2,1,0:T(8,128)(2,1)} %refs_3_.5, ...), custom_call_target="tpu_custom_call" | custom-call | tf_op jit(solution)/shard_map/pallas_call | solution.py:271
  438.4 7.3 %shard_map.86 = (bf16[32,96,2048]{2,1,0:T(8,128)(2,1)}, bf16[32,96,2048]{2,1,0:T(8,128)(2,1)}, f32[8,128]{1,0:T(8,128)S(1)}, bf16[2048,128]{1,0:T(8,128)(2,1)}) custom-call(bf16[30,2,96,2048]{3,2,1,0:T(8,128)(2,1)S(1)} %get-tuple-element.16.refs_0_, bf16[2048,128]{1,0:T(8,128)(2,1)} %get-tuple-element.17.refs_1_), custom_call_target="tpu_custom_call" | custom-call | tf_op jit(solution)/shard_map/pallas_call | solution.py:307
  445.7 72.0 %shard_map.87 = (bf16[6,2,96,2048]{3,2,1,0:T(8,128)(2,1)S(1)}, bf16[6,2,96,256]{3,2,1,0:T(8,128)(2,1)}) custom-call(f32[32,256,768]{2,1,0:T(8,128)} %refs_0_.5, bf16[32,256,768]{2,1,0:T(8,128)(2,1)} %refs_1_.5, f32[32,256,768]{2,1,0:T(8,128)} %refs_2_.5, bf16[32,256,768]{2,1,0:T(8,128)(2,1)} %refs_3_.5, f32[8,128]{1,0:T(8,128)S(1)} %get-tuple-element.18.refs_4_), custom_call_target="tpu_custom_call" | custom-call | tf_op jit(solution)/shard_map/pallas_call | solution.py:271
  517.8 2.3 shard_map.88
  520.1 26.1 %shard_map.89 = (bf16[2,2,96,2048]{3,2,1,0:T(8,128)(2,1)S(1)}, bf16[2,2,96,256]{3,2,1,0:T(8,128)(2,1)}) custom-call(f32[32,256,768]{2,1,0:T(8,128)} %refs_0_.5, bf16[32,256,768]{2,1,0:T(8,128)(2,1)} %refs_1_.5, f32[32,256,768]{2,1,0:T(8,128)} %refs_2_.5, bf16[32,256,768]{2,1,0:T(8,128)(2,1)} %refs_3_.5, f32[8,128]{1,0:T(8,128)S(1)} %get-tuple-element.22.refs_4_), custom_call_target="tpu_custom_call" | custom-call | tf_op jit(solution)/shard_map/pallas_call | solution.py:271
  546.2 1.2 shard_map.90

commit v5 on v4

--- a/solution.py
+++ b/solution.py
@@ -9,7 +9,7 @@
 
 MESH = pl.DeviceIdType.MESH
 SLOTS = 3
-LATE = ((6, 2), (2, 0))
+LATE = ((6, 3), (2, 0))
 EXCHANGE_VMEM = 38 * 2**20
 UNLOAD_VMEM = 4 * 2**20
 

time: 548 us -> 548 us (level)
  no operation moved by 1% of the time
where the time goes in v5:
time: 548 us
  Pallas kernels  547 us (100%)
    pallas_call x3, Pallas kernels, exchange(): pl.pallas_call(functools.partial(exchange_kernel, n, groups, phase), out_...  536 us

profile of v5, /device:TPU:14, one launch (start us, length us, event | category | flops | bytes accessed | tf_op | source)
XLA Modules:
  0.0 547.6 jit_solution(6087575826167986690)
XLA Ops:
  0.6 433.5 %shard_map.85 = (bf16[29,2,96,2048]{3,2,1,0:T(8,128)(2,1)S(1)}, bf16[29,2,96,256]{3,2,1,0:T(8,128)(2,1)}, bf16[2048,128]{1,0:T(8,128)(2,1)}) custom-call(f32[32,256,768]{2,1,0:T(8,128)} %refs_0_.5, bf16[32,256,768]{2,1,0:T(8,128)(2,1)} %refs_1_.5, f32[32,256,768]{2,1,0:T(8,128)} %refs_2_.5, bf16[32,256,768]{2,1,0:T(8,128)(2,1)} %refs_3_.5, ...), custom_call_target="tpu_custom_call" | custom-call | tf_op jit(solution)/shard_map/pallas_call | solution.py:271
  434.1 7.3 %shard_map.86 = (bf16[32,96,2048]{2,1,0:T(8,128)(2,1)}, bf16[32,96,2048]{2,1,0:T(8,128)(2,1)}, f32[8,128]{1,0:T(8,128)S(1)}, bf16[2048,128]{1,0:T(8,128)(2,1)}) custom-call(bf16[29,2,96,2048]{3,2,1,0:T(8,128)(2,1)S(1)} %get-tuple-element.16.refs_0_, bf16[2048,128]{1,0:T(8,128)(2,1)} %get-tuple-element.17.refs_1_), custom_call_target="tpu_custom_call" | custom-call | tf_op jit(solution)/shard_map/pallas_call | solution.py:307
  441.4 80.8 %shard_map.87 = (bf16[6,2,96,2048]{3,2,1,0:T(8,128)(2,1)S(1)}, bf16[6,2,96,256]{3,2,1,0:T(8,128)(2,1)}) custom-call(f32[32,256,768]{2,1,0:T(8,128)} %refs_0_.5, bf16[32,256,768]{2,1,0:T(8,128)(2,1)} %refs_1_.5, f32[32,256,768]{2,1,0:T(8,128)} %refs_2_.5, bf16[32,256,768]{2,1,0:T(8,128)(2,1)} %refs_3_.5, f32[8,128]{1,0:T(8,128)S(1)} %get-tuple-element.18.refs_4_), custom_call_target="tpu_custom_call" | custom-call | tf_op jit(solution)/shard_map/pallas_call | solution.py:271
  522.3 2.3 shard_map.88
  524.6 21.9 %shard_map.89 = (bf16[2,2,96,2048]{3,2,1,0:T(8,128)(2,1)S(1)}, bf16[2,2,96,256]{3,2,1,0:T(8,128)(2,1)}) custom-call(f32[32,256,768]{2,1,0:T(8,128)} %refs_0_.5, bf16[32,256,768]{2,1,0:T(8,128)(2,1)} %refs_1_.5, f32[32,256,768]{2,1,0:T(8,128)} %refs_2_.5, bf16[32,256,768]{2,1,0:T(8,128)(2,1)} %refs_3_.5, f32[8,128]{1,0:T(8,128)S(1)} %get-tuple-element.22.refs_4_), custom_call_target="tpu_custom_call" | custom-call | tf_op jit(solution)/shard_map/pallas_call | solution.py:271
  546.4 1.2 shard_map.90

commit v6 on v4

--- a/solution.py
+++ b/solution.py
@@ -74,7 +74,7 @@
         half = n // 2
         lower = me < half
         near = [lax.rem(me + j, half) + jnp.where(lower, 0, half) for j in range(1, half)]
-        far = [j + jnp.where(lower, half, 0) for j in range(half)]
+        far = [jnp.where(lower, j + half if j % 2 == 0 else n - j, j) for j in range(half)]
 
         def remote(src, dst, e, peer):
             return pltpu.make_async_remote_copy(

time: 548 us -> 548 us (level)
  no operation moved by 1% of the time
where the time goes in v6:
time: 548 us
  Pallas kernels  547 us (100%)
    pallas_call x3, Pallas kernels, exchange(): pl.pallas_call(functools.partial(exchange_kernel, n, groups, phase), out_...  536 us

profile of v6, /device:TPU:14, one launch (start us, length us, event | category | flops | bytes accessed | tf_op | source)
XLA Modules:
  0.0 547.6 jit_solution(6648647088055480934)
XLA Ops:
  0.6 438.0 %shard_map.85 = (bf16[30,2,96,2048]{3,2,1,0:T(8,128)(2,1)S(1)}, bf16[30,2,96,256]{3,2,1,0:T(8,128)(2,1)}, bf16[2048,128]{1,0:T(8,128)(2,1)}) custom-call(f32[32,256,768]{2,1,0:T(8,128)} %refs_0_.5, bf16[32,256,768]{2,1,0:T(8,128)(2,1)} %refs_1_.5, f32[32,256,768]{2,1,0:T(8,128)} %refs_2_.5, bf16[32,256,768]{2,1,0:T(8,128)(2,1)} %refs_3_.5, ...), custom_call_target="tpu_custom_call" | custom-call | tf_op jit(solution)/shard_map/pallas_call | solution.py:271
  438.6 7.3 %shard_map.86 = (bf16[32,96,2048]{2,1,0:T(8,128)(2,1)}, bf16[32,96,2048]{2,1,0:T(8,128)(2,1)}, f32[8,128]{1,0:T(8,128)S(1)}, bf16[2048,128]{1,0:T(8,128)(2,1)}) custom-call(bf16[30,2,96,2048]{3,2,1,0:T(8,128)(2,1)S(1)} %get-tuple-element.16.refs_0_, bf16[2048,128]{1,0:T(8,128)(2,1)} %get-tuple-element.17.refs_1_), custom_call_target="tpu_custom_call" | custom-call | tf_op jit(solution)/shard_map/pallas_call | solution.py:307
  446.0 67.1 %shard_map.87 = (bf16[6,2,96,2048]{3,2,1,0:T(8,128)(2,1)S(1)}, bf16[6,2,96,256]{3,2,1,0:T(8,128)(2,1)}) custom-call(f32[32,256,768]{2,1,0:T(8,128)} %refs_0_.5, bf16[32,256,768]{2,1,0:T(8,128)(2,1)} %refs_1_.5, f32[32,256,768]{2,1,0:T(8,128)} %refs_2_.5, bf16[32,256,768]{2,1,0:T(8,128)(2,1)} %refs_3_.5, f32[8,128]{1,0:T(8,128)S(1)} %get-tuple-element.18.refs_4_), custom_call_target="tpu_custom_call" | custom-call | tf_op jit(solution)/shard_map/pallas_call | solution.py:271
  513.1 2.3 shard_map.88
  515.4 31.0 %shard_map.89 = (bf16[2,2,96,2048]{3,2,1,0:T(8,128)(2,1)S(1)}, bf16[2,2,96,256]{3,2,1,0:T(8,128)(2,1)}) custom-call(f32[32,256,768]{2,1,0:T(8,128)} %refs_0_.5, bf16[32,256,768]{2,1,0:T(8,128)(2,1)} %refs_1_.5, f32[32,256,768]{2,1,0:T(8,128)} %refs_2_.5, bf16[32,256,768]{2,1,0:T(8,128)(2,1)} %refs_3_.5, f32[8,128]{1,0:T(8,128)S(1)} %get-tuple-element.22.refs_4_), custom_call_target="tpu_custom_call" | custom-call | tf_op jit(solution)/shard_map/pallas_call | solution.py:271
  546.4 1.2 shard_map.90
